TPU v7x, 512 devices: a 8x2x16 block of a 8x8x16 slice. The times are simulated.
512 devices in a mesh: groups: 2 (over y), ctx: 32 (over z, core), tp: 8 (over x).
Axes of the slice: x: 8, y: 2, z: 16, core: 2. Of those that a mesh axis runs over, the one named last changes fastest.
The devices are a block of a 8x8x16 slice.
Arguments:
- query_matrix: bfloat16 [8192, 8192], P(('groups', 'ctx'), 'tp'), parts along dimension 0, may hold values from -20 to 20
- key_matrix: bfloat16 [8192, 1024], P(('groups', 'ctx'), 'tp'), parts along dimension 0, may hold values from -20 to 20
- value_matrix: bfloat16 [8192, 1024], P(('groups', 'ctx'), 'tp'), parts along dimension 0, may hold values from -6 to 6
- doc_ids: int32 [8192], P('groups'), parts along dimension 0, may hold values from 0 to 5, never falling along the last dimension, each value on 1 to 2048 neighbouring positions
- out_weight: bfloat16 [8192, 4096], P('tp', 'ctx'), may hold values from -0.0625 to 0.0625
Outputs:
- projected: bfloat16 [8192, 4096], P(('groups', 'ctx'), 'tp'), parts along dimension 0
There are 2 independent parts, one for each index of `groups`. A program takes and returns all parts, laid end to end along the dimension named above; an argument that names none is the same for every part. Nothing has to cross between parts.
Inputs may be any that keep to these rules, and one draw needn't show every extreme that they name: `doc_ids`: non-decreasing along the sequence; each document holds 1 to 2048 tokens, one exactly 2048.
All inputs are finite; a program needn't handle non-finite values.
Results may differ from a plain program's by a relative error of at most 0.015.
Values may be sent and summed in bfloat16 or wider, within the bound.
No kernel may reach another device: no remote copies, remote signals or barrier semaphores. Data moves between devices by JAX's collectives and lax.ppermute only.
A program may use at most 64 MiB of HBM per device.

v0:
```python
import math
import jax
import jax.numpy as jnp
from jax import lax
from jax.sharding import PartitionSpec as P

HEAD_SIZE = 128
rope_base = 1000000.0


def in_one_piece(arrays, axis, dim, along):
    ends, at = ([], 0)
    for a in arrays[:-1]:
        at += a.shape[along]
        ends.append(at)
    both = jnp.concatenate(arrays, axis=along)
    return tuple(jnp.split(lax.all_gather(both, axis, axis=dim, tiled=True), ends, axis=along))


def split_up(x, dim, size):
    lengths = x.shape
    pieces = x.reshape(*lengths[:dim], size, lengths[dim] // size, *lengths[dim + 1 :])
    return jnp.moveaxis(pieces, dim, 0)


def sent_and_summed(x, axis, dim):
    pieces = split_up(x, dim, lax.axis_size(axis))
    arrived = lax.all_to_all(pieces, axis, split_axis=0, concat_axis=0, tiled=True)
    return arrived.astype(jnp.float32).sum(axis=0)


def rotary_tables(rows, token_positions, heads):
    half_dim = HEAD_SIZE // 2
    frequency = jnp.power(
        jnp.float32(rope_base), -jnp.arange(half_dim, dtype=jnp.float32) * (2.0 / HEAD_SIZE)
    )
    angles = token_positions.astype(jnp.float32)[:, None] * frequency[None, :]
    cosine = jnp.cos(angles)[:, None, :]
    sine = jnp.sin(angles)[:, None, :]
    values = rows.astype(jnp.float32).reshape(rows.shape[0], heads, HEAD_SIZE)
    first = values[..., :half_dim]
    second = values[..., half_dim:]
    turned = jnp.concatenate([first * cosine - second * sine, second * cosine + first * sine], -1)
    return turned.reshape(rows.shape[0], heads * HEAD_SIZE).astype(jnp.bfloat16)


def keep_state(held_state, unused_block):
    return held_state


def on_device(query_matrix, key_matrix, value_matrix, doc_ids, out_weight):
    ctx_index = lax.axis_index("ctx")
    tok_rows = query_matrix.shape[0]
    query_heads = query_matrix.shape[1] // HEAD_SIZE
    key_heads = key_matrix.shape[1] // HEAD_SIZE
    group_width = query_heads // key_heads
    inverse_root = HEAD_SIZE ** (-0.5)
    local_rows = jnp.arange(tok_rows, dtype=jnp.int32)
    given_pos = ctx_index * tok_rows + local_rows
    query_matrix_rot = rotary_tables(query_matrix, given_pos, query_heads)
    keys_here = rotary_tables(key_matrix, given_pos, key_heads)
    query_doc = jnp.take(doc_ids, given_pos, axis=0)
    query_four = query_matrix_rot.reshape(tok_rows, key_heads, group_width, HEAD_SIZE)
    first_doc = jnp.min(query_doc)
    last_doc = jnp.max(query_doc)
    last_pos = jnp.max(given_pos)

    def attend(state, block):
        key_block, value_block, doc_block, pos_block = block
        row_max, totals, accum = state
        scores = (
            jnp.einsum("qkgd,skd->kgqs", query_four, key_block, preferred_element_type=jnp.float32)
            * inverse_root
        )
        allowed = (
            (query_doc[:, None] == doc_block[None, :]) & (pos_block[None, :] <= given_pos[:, None])
        )[None, None]
        new_max = jnp.maximum(row_max, jnp.max(jnp.where(allowed, scores, -1e30), -1))
        weights = jnp.where(allowed, jnp.exp(scores - new_max[..., None]), 0.0)
        factor = jnp.exp(row_max - new_max)
        totals = totals * factor + jnp.sum(weights, -1)
        accum = accum * jnp.transpose(factor, (2, 0, 1))[..., None] + jnp.einsum(
            "kgqs,skd->qkgd",
            weights.astype(jnp.bfloat16),
            value_block,
            preferred_element_type=jnp.float32,
        )
        return (new_max, totals, accum)

    start_state = (
        jnp.full((key_heads, group_width, tok_rows), -1e30, jnp.float32),
        jnp.zeros((key_heads, group_width, tok_rows), jnp.float32),
        jnp.zeros((tok_rows, key_heads, group_width, HEAD_SIZE), jnp.float32),
    )
    key_piece, value_piece = in_one_piece((keys_here, value_matrix), "ctx", 0, 1)
    count = key_piece.shape[0]
    block_rows = math.gcd(count, 512)
    block_count = count // block_rows
    positions = jnp.arange(count, dtype=jnp.int32)
    blocks = (
        key_piece.reshape(block_count, block_rows, key_heads, HEAD_SIZE),
        value_piece.reshape(block_count, block_rows, key_heads, HEAD_SIZE),
        jnp.take(doc_ids, positions, axis=0).reshape(block_count, block_rows),
        positions.reshape(block_count, block_rows),
    )

    def step_block(inner_state, block):
        live = (
            (jnp.min(block[3]) <= last_pos)
            & (jnp.min(block[2]) <= last_doc)
            & (jnp.max(block[2]) >= first_doc)
        )
        return (lax.cond(live, attend, keep_state, inner_state, block), None)

    final_state, unused_out = lax.scan(step_block, start_state, blocks)
    row_max, totals, accum = final_state
    attention = (
        (accum / jnp.transpose(totals, (2, 0, 1))[..., None])
        .reshape(tok_rows, query_heads * HEAD_SIZE)
        .astype(jnp.bfloat16)
    )
    terms = jnp.dot(
        attention,
        lax.all_gather(out_weight, "ctx", axis=1, tiled=True),
        preferred_element_type=jnp.float32,
    )
    return sent_and_summed(terms.astype(jnp.bfloat16), "tp", 1).astype(jnp.bfloat16)


def solution(mesh):
    in_specs = (
        P(("groups", "ctx"), "tp"),
        P(("groups", "ctx"), "tp"),
        P(("groups", "ctx"), "tp"),
        P("groups"),
        P("tp", "ctx"),
    )
    out_specs = P(("groups", "ctx"), "tp")
    return jax.shard_map(
        on_device, mesh=mesh, in_specs=in_specs, out_specs=out_specs, check_vma=False
    )
```

profile of v0, /device:TPU:65, one launch (start us, length us, event | category | flops | bytes accessed | tf_op | source)
XLA Modules:
  0.0 262.6 jit_solution(11426903617318993670)
XLA Ops:
  7.2 0.9 copy.19
  8.1 0.9 copy.20
  9.9 0.7 all-gather.5.cloned.1.call-update
  10.7 1.1 copy.21
  12.4 1.1 gather_fusion.1
  13.5 23.0 %gather_fusion = s32[4096]{0:T(1024)S(1)} fusion(s32[4096]{0:T(1024)S(1)} %copy-done, s32[4096]{0:T(1024)S(1)} %iota_clamp_fusion), kind=kCustom, calls=%fused_computation | custom fusion | bytes 49152 | tf_op jit(solution)/shard_map/jit(_take)/gather | solution.py:103
  36.6 0.7 fusion.39
  37.3 82.9 %all-gather.3.cloned.1.call-done = bf16[4096,256]{0,1:T(8,128)(2,1)} async-done(((bf16[128,256]{0,1:T(8,128)(2,1)}), bf16[4096,256]{0,1:T(8,128)(2,1)}) %all-gather.3.cloned.1.call-update) | async-done | bytes 2097168 | tf_op jit(solution)/shard_map/all_gather | solution.py:17
  120.2 1.7 fusion.41
  121.9 0.7 copy.22
  123.8 37.2 %while.15 = (s32[]{:T(128)}, f32[1,8,128]{2,1,0:T(8,128)S(1)}, f32[1,8,128]{2,1,0:T(8,128)S(1)}, f32[128,1,8,128]{0,3,2,1:T(8,128)S(1)}, s32[8,512]{1,0:T(8,128)...) while((s32[]{:T(128)}, f32[1,8,128]{2,1,0:T(8,128)S(1)}, ...), condition=%wide.region_11.12_spmd.clone, body=%wide.region_3.11_spmd.clone.sunk | while | flops 274666112 | bytes 8207207 | solution.py:115
  123.9 0.7 fusion.45
  128.2 1.8 conditional.3
  130.1 0.7 fusion.45
  134.5 0.7 fusion.45
  138.9 0.7 fusion.45
  143.3 0.7 fusion.45
  147.8 0.7 fusion.45
  152.2 0.7 fusion.45
  156.6 0.7 fusion.45
  161.1 54.5 %all-gather.5.cloned.1.call-done = bf16[1024,4096]{1,0:T(8,128)(2,1)} async-done(((bf16[1024,128]{1,0:T(8,128)(2,1)}), bf16[1024,4096]{1,0:T(8,128)(2,1)}) %all-gather.5.cloned.1.call-update) | async-done | bytes 8388624 | tf_op jit(solution)/shard_map/all_gather | solution.py:124
  215.6 4.7 %convolution_convert_fusion = bf16[128,4096]{1,0:T(8,128)(2,1)S(1)} fusion(bf16[128,1024]{0,1:T(8,128)(2,1)S(1)} %bitcast.90, bf16[1024,4096]{1,0:T(8,128)(2,1)} %all-gather.5.cloned.1.call-done), kind=kOutput, calls=%fused_computation.35 | convolution fusion | flops 1074266112 | bytes 9699328 | tf_op jit(solution)/shard_map/dot_general | solution.py:122
  220.3 34.6 %all_to_all.5 = bf16[8,128,512]{2,1,0:T(8,128)(2,1)S(1)} all-to-all(bf16[8,128,512]{2,1,0:T(8,128)(2,1)S(1)} %bitcast.85), channel_id=1, replica_groups=mesh['groups'=2,'ctx'=32,'tp'=8] {'tp'}, dimensions={0} | all-to-all | bytes 2097152 | tf_op jit(solution)/shard_map/all_to_all | solution.py:28
  254.9 0.8 reduce_sum.23
  (51 shorter events, 5.4 us)
Async XLA Ops:
  6.5 5.8 %copy-start = (s32[4096]{0:T(1024)S(1)}, s32[4096]{0:T(1024)}, u32[]{:S(2)}) copy-start(s32[4096]{0:T(1024)} %param.12) | copy-start | bytes 49156
  6.6 113.7 %all-gather.3.cloned.1.call-start = ((), (), s32[]{:S(2)}) async-start(), calls=%async_computation.1 | async-start | bytes 2162688 | tf_op jit(solution)/shard_map/all_gather | solution.py:17
  9.9 205.7 %all-gather.5.cloned.1.call-start = ((), (), s32[]{:S(2)}) async-start(), calls=%async_computation.2 | async-start | bytes 8650752 | tf_op jit(solution)/shard_map/all_gather | solution.py:124
Sparse Core Ops, SparseCore 0:
  10.0 110.2 all-gather.2
  122.3 93.2 all-gather.4
where the time goes:
time: 263 us
  waiting for transfers between devices  138 us (52%)
  blocking collectives  34.6 us (13%)
  local copies, waits for them, and re-layouts  30.9 us (12%)
  loops' own time  29.9 us (11%)
  between operations  13.6 us (5%)
  other arithmetic  9.57 us (4%)
  matrix products  5.76 us (2%)
    all_gather x1, waiting for transfers between devices, in_one_piece(): lax.all_gather(both, axis, axis=dim, tiled=True)  82.9 us
    all_gather x1, waiting for transfers between devices, on_device(): lax.all_gather(out_weight, 'ctx', axis=1, tiled=True)  54.5 us
    all_to_all x1, blocking collectives, sent_and_summed(): lax.all_to_all(pieces, axis, split_axis=0, concat_axis=0, tiled=True)  34.6 us
    another operation x1, loops' own time, on_device(): final_state, unused_out = lax.scan(step_block, start_state, blocks)  29.7 us
    gather x2, local copies, waits for them, and re-layouts, on_device(): jnp.take(doc_ids, positions, axis=0).reshape(block_count, block_rows)  23 us
    reduce_max x8, other arithmetic, step_block(): jnp.max(block[2]) >= first_doc  5.52 us
  transfers between devices with their start and end apart: 2, of which 2 were waited for; matrix products, arithmetic and copies ran while one was open for 14% of the time, Pallas kernels for 0%

commit v1 on v0

--- a/solution.py
+++ b/solution.py
@@ -121,7 +121,9 @@
     )
     terms = jnp.dot(
         attention,
-        lax.all_gather(out_weight, "ctx", axis=1, tiled=True),
+        jnp.concatenate(
+            lax.all_to_all(jnp.stack([out_weight] * lax.axis_size("ctx")), "ctx", 0, 0), axis=1
+        ),
         preferred_element_type=jnp.float32,
     )
     return sent_and_summed(terms.astype(jnp.bfloat16), "tp", 1).astype(jnp.bfloat16)

time: 263 us -> 484 us (1.84); the launches traced: 263 us -> 477 us
  waiting for transfers between devices: 138 us -> 302 us
  starting transfers between devices: 0.07 us -> 46.3 us
    all_to_all x0 -> x1, waiting for transfers between devices: none -> 178 us  [on_device(): lax.all_to_all(jnp.stack([out_weight] * lax.axis_size('ctx')), 'ctx', 0, 0)]
    all_gather x1 -> x0, waiting for transfers between devices: 54.5 us -> none  [on_device(): lax.all_gather(out_weight, 'ctx', axis=1, tiled=True)]
    all_to_all x0 -> x1, starting transfers between devices: none -> 46.3 us  [on_device(): lax.all_to_all(jnp.stack([out_weight] * lax.axis_size('ctx')), 'ctx', 0, 0)]
    all_gather x1, waiting for transfers between devices: 82.9 us -> 125 us  [in_one_piece(): lax.all_gather(both, axis, axis=dim, tiled=True)]
  transfers between devices with their start and end apart: 2 -> 2, of which waited for: 2 -> 2; matrix products, arithmetic and copies ran while one was open for 14% -> 8% of each run, Pallas kernels for 0% -> 0%
where the time goes in v1:
time: 484 us; the launch traced here: 477 us
  waiting for transfers between devices  302 us (62%)
  starting transfers between devices  46.3 us (10%)
  local copies, waits for them, and re-layouts  33.8 us (7%)
  blocking collectives  33.7 us (7%)
  loops' own time  29.5 us (6%)
  between operations  13.7 us (3%)
  other arithmetic  9.82 us (2%)
  matrix products  7.38 us (2%)
    all_to_all x1, waiting for transfers between devices, on_device(): lax.all_to_all(jnp.stack([out_weight] * lax.axis_size('ctx')), 'ctx', 0, 0)  178 us
    all_gather x1, waiting for transfers between devices, in_one_piece(): lax.all_gather(both, axis, axis=dim, tiled=True)  125 us
    all_to_all x1, starting transfers between devices, on_device(): lax.all_to_all(jnp.stack([out_weight] * lax.axis_size('ctx')), 'ctx', 0, 0)  46.3 us
    all_to_all x1, blocking collectives, sent_and_summed(): lax.all_to_all(pieces, axis, split_axis=0, concat_axis=0, tiled=True)  33.7 us
    another operation x1, loops' own time, on_device(): final_state, unused_out = lax.scan(step_block, start_state, blocks)  29.4 us
    gather x2, local copies, waits for them, and re-layouts, on_device(): jnp.take(doc_ids, positions, axis=0).reshape(block_count, block_rows)  23 us
  transfers between devices with their start and end apart: 2, of which 2 were waited for; matrix products, arithmetic and copies ran while one was open for 8% of the time, Pallas kernels for 0%

profile of v1, /device:TPU:65, one launch (start us, length us, event | category | flops | bytes accessed | tf_op | source)
XLA Modules:
  0.0 476.6 jit_solution(9979901134041676084)
XLA Ops:
  6.6 1.1 copy.28
  7.7 4.3 stack.2
  11.9 46.3 %all-to-all-start = ((bf16[32,1024,128]{1,2,0:T(8,128)(2,1)}), bf16[32,1024,128]{1,2,0:T(8,128)(2,1)}, u32[]{:S(2)}, u32[]{:S(2)}) async-start(bf16[32,1024,128]{1,2,0:T(8,128)(2,1)} %stack.2), calls=%async_computation | async-start | bytes 16777216 | tf_op jit(solution)/shard_map/all_to_all | solution.py:125
  60.2 1.1 gather_fusion.1
  61.4 23.0 %gather_fusion = s32[4096]{0:T(1024)S(1)} fusion(s32[4096]{0:T(1024)S(1)} %copy-done, s32[4096]{0:T(1024)S(1)} %iota_clamp_fusion), kind=kCustom, calls=%fused_computation | custom fusion | bytes 49152 | tf_op jit(solution)/shard_map/jit(_take)/gather | solution.py:103
  85.1 0.6 fusion.39
  85.8 124.6 %all-gather.2.cloned.1.call-done = bf16[4096,256]{0,1:T(8,128)(2,1)} async-done(((bf16[128,256]{0,1:T(8,128)(2,1)}), bf16[4096,256]{0,1:T(8,128)(2,1)}) %all-gather.2.cloned.1.call-update) | async-done | bytes 2097168 | tf_op jit(solution)/shard_map/all_gather | solution.py:17
  210.4 1.7 fusion.41
  212.1 0.7 copy.24
  213.3 0.7 copy.31
  214.0 37.1 %while.15 = (s32[]{:T(128)}, f32[1,8,128]{2,1,0:T(8,128)S(1)}, f32[1,8,128]{2,1,0:T(8,128)S(1)}, f32[128,1,8,128]{0,3,2,1:T(8,128)S(1)}, s32[8,512]{1,0:T(8,128)...) while((s32[]{:T(128)}, f32[1,8,128]{2,1,0:T(8,128)S(1)}, ...), condition=%wide.region_11.12_spmd.clone, body=%wide.region_3.11_spmd.clone.sunk | while | flops 274666112 | bytes 8207215 | solution.py:115
  214.1 0.7 fusion.45
  218.4 1.8 conditional.3
  220.3 0.7 fusion.45
  224.7 0.7 fusion.45
  229.1 0.7 fusion.45
  233.5 0.7 fusion.45
  237.9 0.7 fusion.45
  242.4 0.7 fusion.45
  246.8 0.7 fusion.45
  251.2 177.6 %all-to-all-done = bf16[32,1024,128]{1,2,0:T(8,128)(2,1)} async-done(((bf16[32,1024,128]{1,2,0:T(8,128)(2,1)}), bf16[32,1024,128]{1,2,0:T(8,128)(2,1)}, u32[]{:S(2)}, u32[]{:S(2)}) %all-to-all-start) | async-done | bytes 8388640 | tf_op jit(solution)/shard_map/all_to_all | solution.py:125
  428.9 6.3 %convolution_convert_fusion = bf16[128,4096]{1,0:T(8,128)(2,1)S(1)} fusion(bf16[128,1024]{0,1:T(8,128)(2,1)S(1)} %bitcast.93, bf16[1024,4096]{0,1:T(8,128)(2,1)} %bitcast.32), kind=kOutput, calls=%fused_computation.35 | convolution fusion | flops 1074266112 | bytes 9699328 | tf_op jit(solution)/shard_map/dot_general | solution.py:122
  435.2 33.7 %all_to_all.10 = bf16[8,128,512]{2,1,0:T(8,128)(2,1)S(1)} all-to-all(bf16[8,128,512]{2,1,0:T(8,128)(2,1)S(1)} %bitcast.89), channel_id=1, replica_groups=mesh['groups'=2,'ctx'=32,'tp'=8] {'tp'}, dimensions={0} | all-to-all | bytes 2097152 | tf_op jit(solution)/shard_map/all_to_all | solution.py:28
  468.9 0.8 reduce_sum.23
  (58 shorter events, 5.1 us)
Async XLA Ops:
  6.5 53.6 %copy-start = (s32[4096]{0:T(1024)S(1)}, s32[4096]{0:T(1024)}, u32[]{:S(2)}) copy-start(s32[4096]{0:T(1024)} %param.12) | copy-start | bytes 49156
  11.9 46.4 %copy-start.2 = (bf16[128,128]{1,0:T(8,128)(2,1)S(1)}, bf16[128,128]{1,0:T(8,128)(2,1)}, u32[]{:S(2)}) copy-start(bf16[128,128]{1,0:T(8,128)(2,1)} %param.10) | copy-start | bytes 98308
  11.9 46.5 %copy-start.3 = (bf16[128,128]{1,0:T(8,128)(2,1)S(1)}, bf16[128,128]{1,0:T(8,128)(2,1)}, u32[]{:S(2)}) copy-start(bf16[128,128]{1,0:T(8,128)(2,1)} %param.11) | copy-start | bytes 98308
  11.9 416.9 %all-to-all-start = ((bf16[32,1024,128]{1,2,0:T(8,128)(2,1)}), bf16[32,1024,128]{1,2,0:T(8,128)(2,1)}, u32[]{:S(2)}, u32[]{:S(2)}) async-start(bf16[32,1024,128]{1,2,0:T(8,128)(2,1)} %stack.2), calls=%async_computation | async-start | bytes 16777216 | tf_op jit(solution)/shard_map/all_to_all | solution.py:125
  58.2 152.2 %all-gather.2.cloned.1.call-start = ((), (), s32[]{:S(2)}) async-start(), calls=%async_computation.2 | async-start | bytes 2162688 | tf_op jit(solution)/shard_map/all_gather | solution.py:17
  61.4 23.1 %copy-start.1 = (bf16[128,1024]{1,0:T(8,128)(2,1)S(1)}, bf16[128,1024]{1,0:T(8,128)(2,1)}, u32[]{:S(2)}) copy-start(bf16[128,1024]{1,0:T(8,128)(2,1)} %param.9) | copy-start | bytes 786436
Sparse Core Ops, SparseCore 0:
  61.1 149.2 all-gather.1
